TPU v7x, 32 devices: a whole 2x2x4 slice. The times are simulated.
32 devices in a mesh: tm: 16 (over z, y, core), asset: 2 (over x).
Axes of the slice: x: 2, y: 2, z: 4, core: 2. Of those that a mesh axis runs over, the one named last changes fastest.
Arguments:
- tick_bars: float32 [2, 16, 61440], P('asset', 'tm'), may hold values from -20 to 20
- prior_bars: float32 [2, 16, 6400], P('asset', 'tm'), may hold values from -20 to 20, as said below
Outputs:
- connectedness: float32 [48, 8192], P('tm', 'asset')
Inputs may be any that keep to these rules, and one draw needn't show every extreme that they name: `prior_bars`: bar returns of the same assets.
All inputs are finite; a program needn't handle non-finite values.
Results may differ from a plain program's by a relative error of at most 0.0014.
Values may be sent and summed in bfloat16 or wider, within the bound.
A program may use at most 64 MiB of HBM per device.

v0:
```python
import math
import jax
import jax.numpy as jnp
from jax import lax
from jax.sharding import PartitionSpec as P

ASSETS = 8192
SPAN = 30
STRIDE = 5
WIN_DEV = 3
LEAD = 25
FLOOR_SQUARES = 1.0


def from_behind(x, axis, by):
    size = lax.axis_size(axis)
    pairs = [(i, i + by) for i in range(size) if 0 <= i + by < size]
    return lax.ppermute(x, axis, pairs)


def swapped(block, axis, distance):
    count = lax.axis_size(axis)
    route = []
    for low in range(count):
        high = low | 1 << distance
        if high != low and high < count:
            route += [(low, high), (high, low)]
    return lax.ppermute(block, axis, route)


def window_stack(extended):
    columns = extended.shape[1]
    groups = extended.reshape(-1, STRIDE, columns)
    stacked = jnp.stack(
        [groups[offset : offset + WIN_DEV] for offset in range(SPAN // STRIDE)], axis=1
    )
    values = stacked.reshape(WIN_DEV, SPAN, columns)
    centred = values - jnp.mean(values, axis=1, keepdims=True)
    squares = jnp.sum(centred * centred, axis=1, keepdims=True)
    return (centred * lax.rsqrt(jnp.maximum(squares, FLOOR_SQUARES))).astype(jnp.bfloat16)


def block_magnitude(left_part, right_part, offset, block_rows):
    correlation = lax.dot_general(
        left_part[:, offset : offset + block_rows],
        right_part,
        (((0,), (0,)), ((), ())),
        preferred_element_type=jnp.float32,
    )
    return jnp.abs(correlation.astype(jnp.bfloat16)).astype(jnp.float32)


def row_totals(own_windows, other_windows):
    columns = own_windows.shape[2]
    block_rows = min(1024, columns)

    def row_one_window(operands):
        left_part, right_part = operands
        pieces = [
            jnp.sum(block_magnitude(left_part, right_part, offset, block_rows), axis=1)
            for offset in range(0, columns, block_rows)
        ]
        return jnp.concatenate(pieces)

    return lax.map(row_one_window, (own_windows, other_windows))


def both_totals(own_windows, other_windows):
    columns = own_windows.shape[2]
    block_rows = min(1024, columns)

    def both_one_window(operands):
        left_part, right_part = operands
        pieces = []
        column_total = jnp.zeros((right_part.shape[1],), jnp.float32)
        for offset in range(0, columns, block_rows):
            magnitude = block_magnitude(left_part, right_part, offset, block_rows)
            pieces.append(jnp.sum(magnitude, axis=1))
            column_total = column_total + jnp.sum(magnitude, axis=0)
        return (jnp.concatenate(pieces), column_total)

    return lax.map(both_one_window, (own_windows, other_windows))


def earlier_rows(tail_rows, distance):
    return from_behind(tail_rows, "tm", distance)


def time_block_rows(tick_bars, prior_bars):
    groups = lax.axis_size("tm")
    group_cols = ASSETS // (2 * groups)
    outgoing = tick_bars.reshape(groups, 1, -1)
    arrived = lax.all_to_all(outgoing, "tm", split_axis=0, concat_axis=1, tiled=True)
    block_len = arrived.shape[2] // group_cols
    own_rows = jnp.transpose(arrived.reshape(groups, block_len, group_cols), (1, 0, 2)).reshape(
        block_len, groups * group_cols
    )
    prior_all = lax.all_gather(prior_bars, "tm", axis=1, tiled=True)
    series_prior = jnp.transpose(prior_all.reshape(groups, LEAD, group_cols), (1, 0, 2)).reshape(
        LEAD, groups * group_cols
    )
    reach = (LEAD + block_len - 1) // block_len
    earlier = []
    for distance in range(reach, 0, -1):
        needed = min(block_len, LEAD - (distance - 1) * block_len)
        earlier.append(earlier_rows(own_rows[block_len - needed :], distance))
    history = jnp.concatenate(earlier, axis=0)
    position = lax.axis_index("tm")
    first_row = position * block_len
    padded = jnp.concatenate([series_prior, jnp.zeros_like(series_prior)], axis=0)
    from_prior = lax.dynamic_slice_in_dim(padded, jnp.minimum(first_row, LEAD), LEAD, 0)
    before_start = first_row - LEAD + jnp.arange(LEAD, dtype=jnp.int32) < 0
    history = jnp.where(before_start[:, None], from_prior, history)
    return jnp.concatenate([history, own_rows], axis=0)


def shards(tick_bars, prior_bars):
    extended = time_block_rows(tick_bars, prior_bars)
    scaled = window_stack(extended)
    columns = scaled.shape[2]
    empty = jnp.zeros((WIN_DEV, columns), jnp.float32)
    partner = swapped(scaled, "asset", 0)
    tile_index = lax.axis_index("asset")
    quarter = columns // 2
    diagonal_part = row_totals(scaled, scaled)
    column_part = empty
    cross_rows = []
    for half_index in range(2):
        mine = scaled[:, :, half_index * quarter : (half_index + 1) * quarter]
        target = (half_index + tile_index) % 2
        theirs = lax.dynamic_slice_in_dim(partner, target * quarter, quarter, 2)
        row_add, column_add = both_totals(mine, theirs)
        cross_rows.append(row_add)
        column_part = lax.dynamic_update_slice_in_dim(column_part, column_add, target * quarter, 1)
    returned = swapped(column_part.astype(jnp.bfloat16), "asset", 0).astype(column_part.dtype)
    totals = diagonal_part + jnp.concatenate(cross_rows, axis=1) + returned
    return totals * (math.sqrt(SPAN) / ASSETS)


def solution(mesh):
    in_specs = (P("asset", "tm", None), P("asset", "tm", None))
    out_specs = P("tm", "asset")
    return jax.shard_map(shards, mesh=mesh, in_specs=in_specs, out_specs=out_specs, check_vma=False)
```

profile of v0, /device:TPU:0, one launch (start us, length us, event | category | flops | bytes accessed | tf_op | source)
XLA Modules:
  0.0 132.5 jit_solution(15997069284028944891)
XLA Ops:
  0.0 7.5 %all-to-all-start = ((f32[16,1,3840]{2,1,0:T(1,128)}), f32[16,1,3840]{2,1,0:T(1,128)S(1)}, u32[]{:S(2)}, u32[]{:S(2)}) async-start(f32[16,1,3840]{2,1,0:T(1,128)} %bitcast.93), calls=%async_computation | async-start | bytes 491520 | tf_op jit(solution)/shard_map/all_to_all | solution.py:93
  7.6 9.8 %all-to-all-done = f32[16,1,3840]{2,1,0:T(1,128)S(1)} async-done(((f32[16,1,3840]{2,1,0:T(1,128)}), f32[16,1,3840]{2,1,0:T(1,128)S(1)}, u32[]{:S(2)}, u32[]{:S(2)}) %all-to-all-start) | async-done | bytes 245792 | tf_op jit(solution)/shard_map/all_to_all | solution.py:93
  17.3 0.6 reduce.9
  18.3 1.8 %collective-permute-start.1 = (f32[15,4096]{1,0:T(8,128)S(1)}, f32[15,4096]{1,0:T(8,128)S(1)}, u32[]{:S(2)}, u32[]{:S(2)}) collective-permute-start(f32[15,4096]{1,0:T(8,128)S(1)} %bitcast.86), channel_id=1, source_target_pairs={{0,2},{2,4},{4,6},{6,8},{8,10},{10,12},{12,14},{14,16},{16,18},{18... | collective-permute-start | bytes 737288 | tf_op jit(solution)/shard_map/ppermute | solution.py:18
  20.4 2.5 %collective-permute-start = (f32[10,4096]{1,0:T(8,128)S(1)}, f32[10,4096]{1,0:T(8,128)S(1)}, u32[]{:S(2)}, u32[]{:S(2)}) collective-permute-start(f32[10,4096]{1,0:T(8,128)S(1)} %bitcast.92), channel_id=1, source_target_pairs={{0,4},{2,6},{4,8},{6,10},{8,12},{10,14},{12,16},{14,18},{16,20},{1... | collective-permute-start | bytes 491528 | tf_op jit(solution)/shard_map/ppermute | solution.py:18
  23.0 22.3 %all_gather.3 = f32[1,16,6400]{2,0,1:T(1,128)S(1)} all-gather(f32[1,1,6400]{2,0,1:T(1,128)S(1)} %bitcast.94), channel_id=1, replica_groups=mesh['tm'=16,'asset'=2] {'tm'}, dimensions={1}, use_global_device_ids=true | all-gather | bytes 435200 | tf_op jit(solution)/shard_map/all_gather | solution.py:98
  45.3 1.0 reduce.8
  47.2 1.1 pad_maximum_fusion.3
  48.3 0.8 fusion.25
  49.1 1.7 %stack.22 = f32[3,1,5,4096]{3,2,0,1:T(8,128)} reshape(f32[15,4096]{1,0:T(8,128)} %get-tuple-element.124) | data formatting | bytes 491520 | tf_op jit(solution)/shard_map/stack | solution.py:34
  50.8 1.7 %stack.23 = f32[3,1,5,4096]{3,2,0,1:T(8,128)} reshape(f32[15,4096]{1,0:T(8,128)} %get-tuple-element.123) | data formatting | bytes 491520 | tf_op jit(solution)/shard_map/stack | solution.py:34
  52.6 1.0 stack.24
  53.5 1.0 stack.25
  54.5 1.1 fusion.24
  55.7 1.1 fusion.26
  57.3 1.6 %copy.14 = f32[3,6,5,4096]{3,2,1,0:T(8,128)} copy(f32[3,6,5,4096]{3,2,0,1:T(8,128)S(1)} %get-tuple-element.137) | data formatting | bytes 2949120 | tf_op jit(solution)/shard_map/stack | solution.py:34
  59.4 1.7 %reshape.86 = f32[3,30,4096]{2,1,0:T(8,128)S(1)} reshape(f32[3,6,5,4096]{3,2,1,0:T(8,128)} %copy.14) | data formatting | bytes 2949120 | tf_op jit(solution)/shard_map/reshape | solution.py:37
  61.3 1.6 %collective-permute-start.2 = (bf16[3,30,4096]{2,1,0:T(8,128)(2,1)S(1)}, bf16[3,30,4096]{2,1,0:T(8,128)(2,1)S(1)}, u32[]{:S(2)}, u32[]{:S(2)}) collective-permute-start(bf16[3,30,4096]{2,1,0:T(8,128)(2,1)S(1)} %multiply_convert_fusion), channel_id=1, source_target_pairs={{0,1},{1,0},{2,3},{3,2},{4,5},{5,4},{6,7},{7,6},{8,9},{9,8},{10,11... | collective-permute-start | bytes 2211848 | tf_op jit(solution)/shard_map/ppermute | solution.py:28
  62.9 18.2 %collective-permute-done.2 = bf16[3,30,4096]{2,1,0:T(8,128)(2,1)S(1)} collective-permute-done((bf16[3,30,4096]{2,1,0:T(8,128)(2,1)S(1)}, bf16[3,30,4096]{2,1,0:T(8,128)(2,1)S(1)}, u32[]{:S(2)}, u32[]{:S(2)}) %collective-permute-start.2) | collective-permute-done | bytes 737312 | tf_op jit(solution)/shard_map/ppermute | solution.py:28
  81.3 9.1 %while.35 = (s32[]{:T(128)}, f32[3,2048]{1,0:T(4,128)S(1)}, f32[3,2048]{1,0:T(4,128)S(1)}, bf16[3,30,2048]{2,1,0:T(8,128)(2,1)S(1)}, bf16[3,30,2048]{2,1,0:T(8,128)(2,1)S(1)}, /*index=5*/s32[]{:T(128)}, s32[]{:T(128)}) while((s32[]{:T(128)}, f32[3,2048]{1,0:T(4,128)S(1)}, f32[3,2048]{1,0:T(4,128)S(1)}, bf16[3,30,2048]{2,1,0:T(8,128)(2,1)S(1)}, ...), condition=%wide.region_18.19_spmd, body=%wide.region_13.18_spmd.sunk | while | flops 272627712 | bytes 737377 | solution.py:82
  81.3 1.4 %convert_reduce_fusion.25 = (f32[2048]{0:T(1024)S(1)}, f32[1024]{0:T(1024)S(1)}) fusion(bf16[3,30,2048]{2,1,0:T(8,128)(2,1)S(1)} %get-tuple-element.289, s32[]{:T(128)} %get-tuple-element.278, bf16[30,2048]{1,0:T(8,128)(2,1)S(1)} %dynamic-slice_bitcast_fusion.7), kind=kOutput, calls=%fused_computation.12.clone.1 | convolution fusion | flops 136311808 | bytes 208900 | tf_op jit(solution)/shard_map/while/body/eval_jaxpr/dot_general | solution.py:44
  82.7 1.4 %convert_reduce_fusion.24 = (f32[2048]{0:T(1024)S(1)}, f32[1024]{0:T(1024)S(1)}) fusion(bf16[3,30,2048]{2,1,0:T(8,128)(2,1)S(1)} %get-tuple-element.289, s32[]{:T(128)} %get-tuple-element.278, bf16[30,2048]{1,0:T(8,128)(2,1)S(1)} %dynamic-slice_bitcast_fusion.7), kind=kOutput, calls=%fused_computation.10.clone.1 | convolution fusion | flops 136311808 | bytes 208900 | tf_op jit(solution)/shard_map/while/body/eval_jaxpr/dot_general | solution.py:44
  84.3 1.4 %convert_reduce_fusion.25 = (f32[2048]{0:T(1024)S(1)}, f32[1024]{0:T(1024)S(1)}) fusion(bf16[3,30,2048]{2,1,0:T(8,128)(2,1)S(1)} %get-tuple-element.289, s32[]{:T(128)} %get-tuple-element.278, bf16[30,2048]{1,0:T(8,128)(2,1)S(1)} %dynamic-slice_bitcast_fusion.7), kind=kOutput, calls=%fused_computation.12.clone.1 | convolution fusion | flops 136311808 | bytes 208900 | tf_op jit(solution)/shard_map/while/body/eval_jaxpr/dot_general | solution.py:44
  85.7 1.4 %convert_reduce_fusion.24 = (f32[2048]{0:T(1024)S(1)}, f32[1024]{0:T(1024)S(1)}) fusion(bf16[3,30,2048]{2,1,0:T(8,128)(2,1)S(1)} %get-tuple-element.289, s32[]{:T(128)} %get-tuple-element.278, bf16[30,2048]{1,0:T(8,128)(2,1)S(1)} %dynamic-slice_bitcast_fusion.7), kind=kOutput, calls=%fused_computation.10.clone.1 | convolution fusion | flops 136311808 | bytes 208900 | tf_op jit(solution)/shard_map/while/body/eval_jaxpr/dot_general | solution.py:44
  87.4 1.4 %convert_reduce_fusion.25 = (f32[2048]{0:T(1024)S(1)}, f32[1024]{0:T(1024)S(1)}) fusion(bf16[3,30,2048]{2,1,0:T(8,128)(2,1)S(1)} %get-tuple-element.289, s32[]{:T(128)} %get-tuple-element.278, bf16[30,2048]{1,0:T(8,128)(2,1)S(1)} %dynamic-slice_bitcast_fusion.7), kind=kOutput, calls=%fused_computation.12.clone.1 | convolution fusion | flops 136311808 | bytes 208900 | tf_op jit(solution)/shard_map/while/body/eval_jaxpr/dot_general | solution.py:44
  88.7 1.4 %convert_reduce_fusion.24 = (f32[2048]{0:T(1024)S(1)}, f32[1024]{0:T(1024)S(1)}) fusion(bf16[3,30,2048]{2,1,0:T(8,128)(2,1)S(1)} %get-tuple-element.289, s32[]{:T(128)} %get-tuple-element.278, bf16[30,2048]{1,0:T(8,128)(2,1)S(1)} %dynamic-slice_bitcast_fusion.7), kind=kOutput, calls=%fused_computation.10.clone.1 | convolution fusion | flops 136311808 | bytes 208900 | tf_op jit(solution)/shard_map/while/body/eval_jaxpr/dot_general | solution.py:44
  90.4 9.2 %while.36 = (s32[]{:T(128)}, f32[3,2048]{1,0:T(4,128)S(1)}, f32[3,2048]{1,0:T(4,128)S(1)}, bf16[3,30,2048]{2,1,0:T(8,128)(2,1)S(1)}, bf16[3,30,2048]{2,1,0:T(8,128)(2,1)S(1)}, /*index=5*/s32[]{:T(128)}, s32[]{:T(128)}) while((s32[]{:T(128)}, f32[3,2048]{1,0:T(4,128)S(1)}, f32[3,2048]{1,0:T(4,128)S(1)}, bf16[3,30,2048]{2,1,0:T(8,128)(2,1)S(1)}, ...), condition=%wide.region_24.25_spmd, body=%wide.region_19.24_spmd.sunk | while | flops 272627712 | bytes 737377 | solution.py:82
  90.5 1.4 %convert_reduce_fusion.27 = (f32[2048]{0:T(1024)S(1)}, f32[1024]{0:T(1024)S(1)}) fusion(bf16[3,30,2048]{2,1,0:T(8,128)(2,1)S(1)} %get-tuple-element.268, s32[]{:T(128)} %get-tuple-element.257, bf16[30,2048]{1,0:T(8,128)(2,1)S(1)} %dynamic-slice_bitcast_fusion.8), kind=kOutput, calls=%fused_computation.28.clone.1 | convolution fusion | flops 136311808 | bytes 208900 | tf_op jit(solution)/shard_map/while/body/eval_jaxpr/dot_general | solution.py:44
  91.8 1.4 %convert_reduce_fusion.26 = (f32[2048]{0:T(1024)S(1)}, f32[1024]{0:T(1024)S(1)}) fusion(bf16[3,30,2048]{2,1,0:T(8,128)(2,1)S(1)} %get-tuple-element.268, s32[]{:T(128)} %get-tuple-element.257, bf16[30,2048]{1,0:T(8,128)(2,1)S(1)} %dynamic-slice_bitcast_fusion.8), kind=kOutput, calls=%fused_computation.26.clone.1 | convolution fusion | flops 136311808 | bytes 208900 | tf_op jit(solution)/shard_map/while/body/eval_jaxpr/dot_general | solution.py:44
  93.5 1.4 %convert_reduce_fusion.27 = (f32[2048]{0:T(1024)S(1)}, f32[1024]{0:T(1024)S(1)}) fusion(bf16[3,30,2048]{2,1,0:T(8,128)(2,1)S(1)} %get-tuple-element.268, s32[]{:T(128)} %get-tuple-element.257, bf16[30,2048]{1,0:T(8,128)(2,1)S(1)} %dynamic-slice_bitcast_fusion.8), kind=kOutput, calls=%fused_computation.28.clone.1 | convolution fusion | flops 136311808 | bytes 208900 | tf_op jit(solution)/shard_map/while/body/eval_jaxpr/dot_general | solution.py:44
  94.9 1.4 %convert_reduce_fusion.26 = (f32[2048]{0:T(1024)S(1)}, f32[1024]{0:T(1024)S(1)}) fusion(bf16[3,30,2048]{2,1,0:T(8,128)(2,1)S(1)} %get-tuple-element.268, s32[]{:T(128)} %get-tuple-element.257, bf16[30,2048]{1,0:T(8,128)(2,1)S(1)} %dynamic-slice_bitcast_fusion.8), kind=kOutput, calls=%fused_computation.26.clone.1 | convolution fusion | flops 136311808 | bytes 208900 | tf_op jit(solution)/shard_map/while/body/eval_jaxpr/dot_general | solution.py:44
  96.6 1.4 %convert_reduce_fusion.27 = (f32[2048]{0:T(1024)S(1)}, f32[1024]{0:T(1024)S(1)}) fusion(bf16[3,30,2048]{2,1,0:T(8,128)(2,1)S(1)} %get-tuple-element.268, s32[]{:T(128)} %get-tuple-element.257, bf16[30,2048]{1,0:T(8,128)(2,1)S(1)} %dynamic-slice_bitcast_fusion.8), kind=kOutput, calls=%fused_computation.28.clone.1 | convolution fusion | flops 136311808 | bytes 208900 | tf_op jit(solution)/shard_map/while/body/eval_jaxpr/dot_general | solution.py:44
  97.9 1.4 %convert_reduce_fusion.26 = (f32[2048]{0:T(1024)S(1)}, f32[1024]{0:T(1024)S(1)}) fusion(bf16[3,30,2048]{2,1,0:T(8,128)(2,1)S(1)} %get-tuple-element.268, s32[]{:T(128)} %get-tuple-element.257, bf16[30,2048]{1,0:T(8,128)(2,1)S(1)} %dynamic-slice_bitcast_fusion.8), kind=kOutput, calls=%fused_computation.26.clone.1 | convolution fusion | flops 136311808 | bytes 208900 | tf_op jit(solution)/shard_map/while/body/eval_jaxpr/dot_general | solution.py:44
  99.7 1.6 %collective-permute-start.3 = (bf16[3,4096]{1,0:T(4,128)(2,1)S(1)}, bf16[3,4096]{1,0:T(4,128)(2,1)S(1)}, u32[]{:S(2)}, u32[]{:S(2)}) collective-permute-start(bf16[3,4096]{1,0:T(4,128)(2,1)S(1)} %convert_element_type.58), channel_id=1, source_target_pairs={{0,1},{1,0},{2,3},{3,2},{4,5},{5,4},{6,7},{7,6},{8,9},{9,8},{10,11... | collective-permute-start | bytes 73736 | tf_op jit(solution)/shard_map/ppermute | solution.py:28
  101.3 30.5 %while.34 = (s32[]{:T(128)}, f32[3,4096]{1,0:T(4,128)S(1)}, bf16[3,30,4096]{2,1,0:T(8,128)(2,1)S(1)}, s32[]{:T(128)}, s32[]{:T(128)}) while((s32[]{:T(128)}, f32[3,4096]{1,0:T(4,128)S(1)}, bf16[3,30,4096]{2,1,0:T(8,128)(2,1)S(1)}, s32[]{:T(128)}, s32[]{:T(128)}) %tuple.68), condition=%wide.region_12.13_spmd, body=%wide.region_7.12_spmd.sunk | while | flops 1073750016 | bytes 1884229 | solution.py:65
  101.5 2.4 %convert_reduce_fusion.20 = f32[1024]{0:T(1024)S(1)} fusion(bf16[30,4096]{1,0:T(8,128)(2,1)S(1)} %dynamic-slice_bitcast_fusion.6), kind=kOutput, calls=%fused_computation.clone.1 | convolution fusion | flops 268434432 | bytes 331776 | tf_op jit(solution)/shard_map/while/body/eval_jaxpr/dot_general | solution.py:44
  104.0 2.5 %convert_reduce_fusion.21 = f32[1024]{0:T(1024)S(1)} fusion(bf16[30,4096]{1,0:T(8,128)(2,1)S(1)} %dynamic-slice_bitcast_fusion.6), kind=kOutput, calls=%fused_computation.1.clone.1 | convolution fusion | flops 268434432 | bytes 331776 | tf_op jit(solution)/shard_map/while/body/eval_jaxpr/dot_general | solution.py:44
  106.4 2.5 %convert_reduce_fusion.22 = f32[1024]{0:T(1024)S(1)} fusion(bf16[30,4096]{1,0:T(8,128)(2,1)S(1)} %dynamic-slice_bitcast_fusion.6), kind=kOutput, calls=%fused_computation.2.clone.1 | convolution fusion | flops 268434432 | bytes 331776 | tf_op jit(solution)/shard_map/while/body/eval_jaxpr/dot_general | solution.py:44
  108.9 2.5 %convert_reduce_fusion.23 = f32[1024]{0:T(1024)S(1)} fusion(bf16[30,4096]{1,0:T(8,128)(2,1)S(1)} %dynamic-slice_bitcast_fusion.6), kind=kOutput, calls=%fused_computation.3.clone.1 | convolution fusion | flops 268434432 | bytes 331776 | tf_op jit(solution)/shard_map/while/body/eval_jaxpr/dot_general | solution.py:44
  111.6 2.4 %convert_reduce_fusion.20 = f32[1024]{0:T(1024)S(1)} fusion(bf16[30,4096]{1,0:T(8,128)(2,1)S(1)} %dynamic-slice_bitcast_fusion.6), kind=kOutput, calls=%fused_computation.clone.1 | convolution fusion | flops 268434432 | bytes 331776 | tf_op jit(solution)/shard_map/while/body/eval_jaxpr/dot_general | solution.py:44
  114.1 2.5 %convert_reduce_fusion.21 = f32[1024]{0:T(1024)S(1)} fusion(bf16[30,4096]{1,0:T(8,128)(2,1)S(1)} %dynamic-slice_bitcast_fusion.6), kind=kOutput, calls=%fused_computation.1.clone.1 | convolution fusion | flops 268434432 | bytes 331776 | tf_op jit(solution)/shard_map/while/body/eval_jaxpr/dot_general | solution.py:44
  116.5 2.5 %convert_reduce_fusion.22 = f32[1024]{0:T(1024)S(1)} fusion(bf16[30,4096]{1,0:T(8,128)(2,1)S(1)} %dynamic-slice_bitcast_fusion.6), kind=kOutput, calls=%fused_computation.2.clone.1 | convolution fusion | flops 268434432 | bytes 331776 | tf_op jit(solution)/shard_map/while/body/eval_jaxpr/dot_general | solution.py:44
  119.0 2.5 %convert_reduce_fusion.23 = f32[1024]{0:T(1024)S(1)} fusion(bf16[30,4096]{1,0:T(8,128)(2,1)S(1)} %dynamic-slice_bitcast_fusion.6), kind=kOutput, calls=%fused_computation.3.clone.1 | convolution fusion | flops 268434432 | bytes 331776 | tf_op jit(solution)/shard_map/while/body/eval_jaxpr/dot_general | solution.py:44
  121.7 2.4 %convert_reduce_fusion.20 = f32[1024]{0:T(1024)S(1)} fusion(bf16[30,4096]{1,0:T(8,128)(2,1)S(1)} %dynamic-slice_bitcast_fusion.6), kind=kOutput, calls=%fused_computation.clone.1 | convolution fusion | flops 268434432 | bytes 331776 | tf_op jit(solution)/shard_map/while/body/eval_jaxpr/dot_general | solution.py:44
  124.2 2.5 %convert_reduce_fusion.21 = f32[1024]{0:T(1024)S(1)} fusion(bf16[30,4096]{1,0:T(8,128)(2,1)S(1)} %dynamic-slice_bitcast_fusion.6), kind=kOutput, calls=%fused_computation.1.clone.1 | convolution fusion | flops 268434432 | bytes 331776 | tf_op jit(solution)/shard_map/while/body/eval_jaxpr/dot_general | solution.py:44
  126.6 2.5 %convert_reduce_fusion.22 = f32[1024]{0:T(1024)S(1)} fusion(bf16[30,4096]{1,0:T(8,128)(2,1)S(1)} %dynamic-slice_bitcast_fusion.6), kind=kOutput, calls=%fused_computation.2.clone.1 | convolution fusion | flops 268434432 | bytes 331776 | tf_op jit(solution)/shard_map/while/body/eval_jaxpr/dot_general | solution.py:44
  129.1 2.5 %convert_reduce_fusion.23 = f32[1024]{0:T(1024)S(1)} fusion(bf16[30,4096]{1,0:T(8,128)(2,1)S(1)} %dynamic-slice_bitcast_fusion.6), kind=kOutput, calls=%fused_computation.3.clone.1 | convolution fusion | flops 268434432 | bytes 331776 | tf_op jit(solution)/shard_map/while/body/eval_jaxpr/dot_general | solution.py:44
  131.8 0.7 fusion.22
  (80 shorter events, 5.5 us)
Async XLA Ops:
  0.0 23.0 %copy-start.1 = (f32[1,1,6400]{2,1,0:T(1,128)S(1)}, f32[1,1,6400]{2,1,0:T(1,128)}, u32[]{:S(2)}) copy-start(f32[1,1,6400]{2,1,0:T(1,128)} %param.9) | copy-start | bytes 76804
  0.0 17.3 %all-to-all-start = ((f32[16,1,3840]{2,1,0:T(1,128)}), f32[16,1,3840]{2,1,0:T(1,128)S(1)}, u32[]{:S(2)}, u32[]{:S(2)}) async-start(f32[16,1,3840]{2,1,0:T(1,128)} %bitcast.93), calls=%async_computation | async-start | bytes 491520 | tf_op jit(solution)/shard_map/all_to_all | solution.py:93
  18.3 28.7 %collective-permute-start.1 = (f32[15,4096]{1,0:T(8,128)S(1)}, f32[15,4096]{1,0:T(8,128)S(1)}, u32[]{:S(2)}, u32[]{:S(2)}) collective-permute-start(f32[15,4096]{1,0:T(8,128)S(1)} %bitcast.86), channel_id=1, source_target_pairs={{0,2},{2,4},{4,6},{6,8},{8,10},{10,12},{12,14},{14,16},{16,18},{18... | collective-permute-start | bytes 737288 | tf_op jit(solution)/shard_map/ppermute | solution.py:18
  20.4 26.6 %collective-permute-start = (f32[10,4096]{1,0:T(8,128)S(1)}, f32[10,4096]{1,0:T(8,128)S(1)}, u32[]{:S(2)}, u32[]{:S(2)}) collective-permute-start(f32[10,4096]{1,0:T(8,128)S(1)} %bitcast.92), channel_id=1, source_target_pairs={{0,4},{2,6},{4,8},{6,10},{8,12},{10,14},{12,16},{14,18},{16,20},{1... | collective-permute-start | bytes 491528 | tf_op jit(solution)/shard_map/ppermute | solution.py:18
  57.3 1.6 %copy-start = (f32[3,4096]{1,0:T(4,128)S(1)}, f32[3,4096]{1,0:T(4,128)}, u32[]{:S(2)}) copy-start(f32[3,4096]{1,0:T(4,128)} %get-tuple-element.128) | copy-start | bytes 147460
  61.3 19.9 %collective-permute-start.2 = (bf16[3,30,4096]{2,1,0:T(8,128)(2,1)S(1)}, bf16[3,30,4096]{2,1,0:T(8,128)(2,1)S(1)}, u32[]{:S(2)}, u32[]{:S(2)}) collective-permute-start(bf16[3,30,4096]{2,1,0:T(8,128)(2,1)S(1)} %multiply_convert_fusion), channel_id=1, source_target_pairs={{0,1},{1,0},{2,3},{3,2},{4,5},{5,4},{6,7},{7,6},{8,9},{9,8},{10,11... | collective-permute-start | bytes 2211848 | tf_op jit(solution)/shard_map/ppermute | solution.py:28
  99.7 32.1 %collective-permute-start.3 = (bf16[3,4096]{1,0:T(4,128)(2,1)S(1)}, bf16[3,4096]{1,0:T(4,128)(2,1)S(1)}, u32[]{:S(2)}, u32[]{:S(2)}) collective-permute-start(bf16[3,4096]{1,0:T(4,128)(2,1)S(1)} %convert_element_type.58), channel_id=1, source_target_pairs={{0,1},{1,0},{2,3},{3,2},{4,5},{5,4},{6,7},{7,6},{8,9},{9,8},{10,11... | collective-permute-start | bytes 73736 | tf_op jit(solution)/shard_map/ppermute | solution.py:28
where the time goes:
time: 133 us; the launch traced here: 132 us
  matrix products  45.7 us (34%)
  waiting for transfers between devices  28 us (21%)
  blocking collectives  22.3 us (17%)
  starting transfers between devices  15 us (11%)
  local copies, waits for them, and re-layouts  12.9 us (10%)
  other arithmetic  7.66 us (6%)
    dot_general x24, matrix products, block_magnitude(): lax.dot_general(left_part[:, offset:offset + block_rows], right_part, (((...  45.7 us
    all_gather x1, blocking collectives, time_block_rows(): prior_all = lax.all_gather(prior_bars, 'tm', axis=1, tiled=True)  22.3 us
    ppermute x2, waiting for transfers between devices, swapped(): return lax.ppermute(block, axis, route)  18.2 us
    all_to_all x1, waiting for transfers between devices, time_block_rows(): lax.all_to_all(outgoing, 'tm', split_axis=0, concat_axis=1, tiled=True)  9.75 us
    all_to_all x1, starting transfers between devices, time_block_rows(): lax.all_to_all(outgoing, 'tm', split_axis=0, concat_axis=1, tiled=True)  7.55 us
    another operation x7, local copies, waits for them, and re-layouts, window_stack(): jnp.stack([groups[offset:offset + WIN_DEV] for offset in range(SPAN // ST...  7.1 us
    ppermute x2, starting transfers between devices, from_behind(): return lax.ppermute(x, axis, pairs)  4.3 us
    reduce_sum x6, other arithmetic, window_stack(): centred = values - jnp.mean(values, axis=1, keepdims=True)  3.52 us
  transfers between devices with their start and end apart: 5, of which 2 were waited for; matrix products, arithmetic and copies ran while one was open for 24% of the time, Pallas kernels for 0%

commit v1 on v0

--- a/solution.py
+++ b/solution.py
@@ -10,6 +10,22 @@
 WIN_DEV = 3
 LEAD = 25
 FLOOR_SQUARES = 1.0
+
+
+def gather_around(x, axis, dim):
+    ways, here, step = (lax.axis_size(axis), lax.axis_index(axis), x.shape[dim])
+    shape = [n * ways if d == dim else n for d, n in enumerate(x.shape)]
+    full = lax.dynamic_update_slice_in_dim(jnp.zeros(shape, x.dtype), x, here * step, axis=dim)
+    going_up = going_down = x
+    for far in range(1, ways // 2 + 1):
+        going_up = lax.ppermute(going_up, axis, [(d, (d + 1) % ways) for d in range(ways)])
+        full = lax.dynamic_update_slice_in_dim(full, going_up, (here - far) % ways * step, axis=dim)
+        if 2 * far < ways:
+            going_down = lax.ppermute(going_down, axis, [(d, (d - 1) % ways) for d in range(ways)])
+            full = lax.dynamic_update_slice_in_dim(
+                full, going_down, (here + far) % ways * step, axis=dim
+            )
+    return full
 
 
 def from_behind(x, axis, by):
@@ -95,7 +111,7 @@
     own_rows = jnp.transpose(arrived.reshape(groups, block_len, group_cols), (1, 0, 2)).reshape(
         block_len, groups * group_cols
     )
-    prior_all = lax.all_gather(prior_bars, "tm", axis=1, tiled=True)
+    prior_all = gather_around(prior_bars, "tm", 1)
     series_prior = jnp.transpose(prior_all.reshape(groups, LEAD, group_cols), (1, 0, 2)).reshape(
         LEAD, groups * group_cols
     )

time: 133 us -> 146 us (1.098)
  starting transfers between devices: 15 us -> 44.5 us
  blocking collectives: 22.3 us -> 0 us
  local copies, waits for them, and re-layouts: 12.9 us -> 21.9 us
  waiting for transfers between devices: 28 us -> 25.2 us
    ppermute x0 -> x15, starting transfers between devices: none -> 31.3 us  [the longest x7 30.9 us: gather_around(): lax.ppermute(going_down, axis, [(d, (d - 1) % ways) for d in range(ways)])]
    all_gather x1 -> x0, blocking collectives: 22.3 us -> none  [time_block_rows(): prior_all = lax.all_gather(prior_bars, 'tm', axis=1, tiled=True)]
    ppermute x0 -> x15, waiting for transfers between devices: none -> 11.4 us  [the longest x8 6.78 us: gather_around(): lax.ppermute(going_up, axis, [(d, (d + 1) % ways) for d in range(ways)])]
    dynamic_update_slice x0 -> x16, local copies, waits for them, and re-layouts: none -> 9.97 us  [the longest x8 5.07 us: gather_around(): lax.dynamic_update_slice_in_dim(full, going_up, (here - far) % ways * ste...]
    all_to_all x1, waiting for transfers between devices: 9.75 us -> 0.01 us  [time_block_rows(): lax.all_to_all(outgoing, 'tm', split_axis=0, concat_axis=1, tiled=True)]
    ppermute x2, waiting for transfers between devices: 18.2 us -> 13.9 us  [swapped(): return lax.ppermute(block, axis, route)]
    ppermute x2, starting transfers between devices: 4.3 us -> 2.61 us  [from_behind(): return lax.ppermute(x, axis, pairs)]
  transfers between devices with their start and end apart: 5 -> 20, of which waited for: 2 -> 6; matrix products, arithmetic and copies ran while one was open for 24% -> 29% of each run, Pallas kernels for 0% -> 0%
where the time goes in v1:
time: 146 us; the launch traced here: 145 us
  matrix products  45.7 us (31%)
  starting transfers between devices  44.5 us (30%)
  waiting for transfers between devices  25.2 us (17%)
  local copies, waits for them, and re-layouts  21.9 us (15%)
  other arithmetic  6.6 us (5%)
    dot_general x24, matrix products, block_magnitude(): lax.dot_general(left_part[:, offset:offset + block_rows], right_part, (((...  45.7 us
    ppermute x7, starting transfers between devices, gather_around(): lax.ppermute(going_down, axis, [(d, (d - 1) % ways) for d in range(ways)])  30.9 us
    ppermute x2, waiting for transfers between devices, swapped(): return lax.ppermute(block, axis, route)  13.9 us
    all_to_all x1, starting transfers between devices, time_block_rows(): lax.all_to_all(outgoing, 'tm', split_axis=0, concat_axis=1, tiled=True)  7.41 us
    ppermute x8, waiting for transfers between devices, gather_around(): lax.ppermute(going_up, axis, [(d, (d + 1) % ways) for d in range(ways)])  6.78 us
    another operation x7, local copies, waits for them, and re-layouts, window_stack(): jnp.stack([groups[offset:offset + WIN_DEV] for offset in range(SPAN // ST...  6.15 us
    dynamic_update_slice x8, local copies, waits for them, and re-layouts, gather_around(): lax.dynamic_update_slice_in_dim(full, going_up, (here - far) % ways * ste...  5.07 us
    ppermute x7, waiting for transfers between devices, gather_around(): lax.ppermute(going_down, axis, [(d, (d - 1) % ways) for d in range(ways)])  4.58 us
  transfers between devices with their start and end apart: 20, of which 6 were waited for; matrix products, arithmetic and copies ran while one was open for 29% of the time, Pallas kernels for 0%

profile of v1, /device:TPU:0, one launch (start us, length us, event | category | flops | bytes accessed | tf_op | source)
XLA Modules:
  0.0 145.4 jit_solution(11642380642806564775)
XLA Ops:
  0.0 7.4 %all-to-all-start = ((f32[16,1,3840]{2,1,0:T(1,128)}), f32[16,1,3840]{2,1,0:T(1,128)S(1)}, u32[]{:S(2)}, u32[]{:S(2)}) async-start(f32[16,1,3840]{2,1,0:T(1,128)} %bitcast.92), calls=%async_computation | async-start | bytes 491520 | tf_op jit(solution)/shard_map/all_to_all | solution.py:109
  7.8 4.1 %collective-permute-start.1 = (f32[1,1,6400]{2,1,0:T(1,128)}, f32[1,1,6400]{2,1,0:T(1,128)S(1)}, u32[]{:S(2)}, u32[]{:S(2)}) collective-permute-start(f32[1,1,6400]{2,1,0:T(1,128)} %param.9), channel_id=1, source_target_pairs={{0,30},{2,0},{4,2},{6,4},{8,6},{10,8},{12,10},{14,12},{16,14},{18,... | collective-permute-start | bytes 76808 | tf_op jit(solution)/shard_map/ppermute | solution.py:24
  11.9 5.2 %collective-permute-done = f32[1,1,6400]{2,1,0:T(1,128)S(1)} collective-permute-done((f32[1,1,6400]{2,1,0:T(1,128)}, f32[1,1,6400]{2,1,0:T(1,128)S(1)}, u32[]{:S(2)}, u32[]{:S(2)}) %collective-permute-start) | collective-permute-done | bytes 25632 | tf_op jit(solution)/shard_map/ppermute | solution.py:21
  17.2 4.4 %collective-permute-start.3 = (f32[1,1,6400]{2,1,0:T(1,128)S(1)}, f32[1,1,6400]{2,1,0:T(1,128)S(1)}, u32[]{:S(2)}, u32[]{:S(2)}) collective-permute-start(f32[1,1,6400]{2,1,0:T(1,128)S(1)} %collective-permute-done.1), channel_id=1, source_target_pairs={{0,30},{2,0},{4,2},{6,4},{8,6},{10,8},{12,10},{14,12},{16,14},{18,... | collective-permute-start | bytes 76808 | tf_op jit(solution)/shard_map/ppermute | solution.py:24
  21.6 1.5 %collective-permute-done.2 = f32[1,1,6400]{2,1,0:T(1,128)S(1)} collective-permute-done((f32[1,1,6400]{2,1,0:T(1,128)S(1)}, f32[1,1,6400]{2,1,0:T(1,128)S(1)}, u32[]{:S(2)}, u32[]{:S(2)}) %collective-permute-start.2) | collective-permute-done | bytes 25632 | tf_op jit(solution)/shard_map/ppermute | solution.py:21
  24.2 1.3 collective-permute-start.16
  25.5 4.5 %collective-permute-start.5 = (f32[1,1,6400]{2,1,0:T(1,128)S(1)}, f32[1,1,6400]{2,1,0:T(1,128)S(1)}, u32[]{:S(2)}, u32[]{:S(2)}) collective-permute-start(f32[1,1,6400]{2,1,0:T(1,128)S(1)} %collective-permute-done.3), channel_id=1, source_target_pairs={{0,30},{2,0},{4,2},{6,4},{8,6},{10,8},{12,10},{14,12},{16,14},{18,... | collective-permute-start | bytes 76808 | tf_op jit(solution)/shard_map/ppermute | solution.py:24
  30.0 1.5 %collective-permute-done.5 = f32[1,1,6400]{2,1,0:T(1,128)S(1)} collective-permute-done((f32[1,1,6400]{2,1,0:T(1,128)S(1)}, f32[1,1,6400]{2,1,0:T(1,128)S(1)}, u32[]{:S(2)}, u32[]{:S(2)}) %collective-permute-start.5) | collective-permute-done | bytes 25632 | tf_op jit(solution)/shard_map/ppermute | solution.py:24
  31.5 4.4 %collective-permute-start.7 = (f32[1,1,6400]{2,1,0:T(1,128)S(1)}, f32[1,1,6400]{2,1,0:T(1,128)S(1)}, u32[]{:S(2)}, u32[]{:S(2)}) collective-permute-start(f32[1,1,6400]{2,1,0:T(1,128)S(1)} %collective-permute-done.5), channel_id=1, source_target_pairs={{0,30},{2,0},{4,2},{6,4},{8,6},{10,8},{12,10},{14,12},{16,14},{18,... | collective-permute-start | bytes 76808 | tf_op jit(solution)/shard_map/ppermute | solution.py:24
  35.9 1.5 %collective-permute-done.7 = f32[1,1,6400]{2,1,0:T(1,128)S(1)} collective-permute-done((f32[1,1,6400]{2,1,0:T(1,128)S(1)}, f32[1,1,6400]{2,1,0:T(1,128)S(1)}, u32[]{:S(2)}, u32[]{:S(2)}) %collective-permute-start.7) | collective-permute-done | bytes 25632 | tf_op jit(solution)/shard_map/ppermute | solution.py:24
  37.4 4.4 %collective-permute-start.9 = (f32[1,1,6400]{2,1,0:T(1,128)S(1)}, f32[1,1,6400]{2,1,0:T(1,128)S(1)}, u32[]{:S(2)}, u32[]{:S(2)}) collective-permute-start(f32[1,1,6400]{2,1,0:T(1,128)S(1)} %collective-permute-done.7), channel_id=1, source_target_pairs={{0,30},{2,0},{4,2},{6,4},{8,6},{10,8},{12,10},{14,12},{16,14},{18,... | collective-permute-start | bytes 76808 | tf_op jit(solution)/shard_map/ppermute | solution.py:24
  42.2 1.3 collective-permute-start.15
  43.5 4.5 %collective-permute-start.11 = (f32[1,1,6400]{2,1,0:T(1,128)S(1)}, f32[1,1,6400]{2,1,0:T(1,128)S(1)}, u32[]{:S(2)}, u32[]{:S(2)}) collective-permute-start(f32[1,1,6400]{2,1,0:T(1,128)S(1)} %collective-permute-done.9), channel_id=1, source_target_pairs={{0,30},{2,0},{4,2},{6,4},{8,6},{10,8},{12,10},{14,12},{16,14},{18,... | collective-permute-start | bytes 76808 | tf_op jit(solution)/shard_map/ppermute | solution.py:24
  48.0 1.5 %collective-permute-done.11 = f32[1,1,6400]{2,1,0:T(1,128)S(1)} collective-permute-done((f32[1,1,6400]{2,1,0:T(1,128)S(1)}, f32[1,1,6400]{2,1,0:T(1,128)S(1)}, u32[]{:S(2)}, u32[]{:S(2)}) %collective-permute-start.11) | collective-permute-done | bytes 25632 | tf_op jit(solution)/shard_map/ppermute | solution.py:24
  49.5 4.5 %collective-permute-start.13 = (f32[1,1,6400]{2,1,0:T(1,128)S(1)}, f32[1,1,6400]{2,1,0:T(1,128)S(1)}, u32[]{:S(2)}, u32[]{:S(2)}) collective-permute-start(f32[1,1,6400]{2,1,0:T(1,128)S(1)} %collective-permute-done.11), channel_id=1, source_target_pairs={{0,30},{2,0},{4,2},{6,4},{8,6},{10,8},{12,10},{14,12},{16,14},{18,... | collective-permute-start | bytes 76808 | tf_op jit(solution)/shard_map/ppermute | solution.py:24
  67.3 1.7 %stack.22 = f32[3,1,5,4096]{3,2,0,1:T(8,128)} reshape(f32[15,4096]{1,0:T(8,128)} %get-tuple-element.124) | data formatting | bytes 491520 | tf_op jit(solution)/shard_map/stack | solution.py:50
  74.6 1.6 %copy.15 = f32[3,6,5,4096]{3,2,1,0:T(8,128)} copy(f32[3,6,5,4096]{3,2,0,1:T(8,128)S(1)} %get-tuple-element.137) | data formatting | bytes 2949120 | tf_op jit(solution)/shard_map/stack | solution.py:50
  76.7 1.7 %reshape.86 = f32[3,30,4096]{2,1,0:T(8,128)S(1)} reshape(f32[3,6,5,4096]{3,2,1,0:T(8,128)} %copy.15) | data formatting | bytes 2949120 | tf_op jit(solution)/shard_map/reshape | solution.py:53
  78.6 1.6 %collective-permute-start.17 = (bf16[3,30,4096]{2,1,0:T(8,128)(2,1)S(1)}, bf16[3,30,4096]{2,1,0:T(8,128)(2,1)S(1)}, u32[]{:S(2)}, u32[]{:S(2)}) collective-permute-start(bf16[3,30,4096]{2,1,0:T(8,128)(2,1)S(1)} %multiply_convert_fusion), channel_id=1, source_target_pairs={{0,1},{1,0},{2,3},{3,2},{4,5},{5,4},{6,7},{7,6},{8,9},{9,8},{10,11... | collective-permute-start | bytes 2211848 | tf_op jit(solution)/shard_map/ppermute | solution.py:44
  80.2 13.9 %collective-permute-done.17 = bf16[3,30,4096]{2,1,0:T(8,128)(2,1)S(1)} collective-permute-done((bf16[3,30,4096]{2,1,0:T(8,128)(2,1)S(1)}, bf16[3,30,4096]{2,1,0:T(8,128)(2,1)S(1)}, u32[]{:S(2)}, u32[]{:S(2)}) %collective-permute-start.17) | collective-permute-done | bytes 737312 | tf_op jit(solution)/shard_map/ppermute | solution.py:44
  94.2 9.1 %while.35 = (s32[]{:T(128)}, f32[3,2048]{1,0:T(4,128)S(1)}, f32[3,2048]{1,0:T(4,128)S(1)}, bf16[3,30,2048]{2,1,0:T(8,128)(2,1)S(1)}, bf16[3,30,2048]{2,1,0:T(8,128)(2,1)S(1)}, /*index=5*/s32[]{:T(128)}, s32[]{:T(128)}) while((s32[]{:T(128)}, f32[3,2048]{1,0:T(4,128)S(1)}, f32[3,2048]{1,0:T(4,128)S(1)}, bf16[3,30,2048]{2,1,0:T(8,128)(2,1)S(1)}, ...), condition=%wide.region_18.19_spmd, body=%wide.region_13.18_spmd.sunk | while | flops 272627712 | bytes 737377 | solution.py:98
  94.2 1.4 convert_reduce_fusion.25
  95.5 1.4 convert_reduce_fusion.24
  97.2 1.4 convert_reduce_fusion.25
  98.6 1.4 convert_reduce_fusion.24
  100.3 1.4 convert_reduce_fusion.25
  101.6 1.4 convert_reduce_fusion.24
  103.3 9.2 %while.36 = (s32[]{:T(128)}, f32[3,2048]{1,0:T(4,128)S(1)}, f32[3,2048]{1,0:T(4,128)S(1)}, bf16[3,30,2048]{2,1,0:T(8,128)(2,1)S(1)}, bf16[3,30,2048]{2,1,0:T(8,128)(2,1)S(1)}, /*index=5*/s32[]{:T(128)}, s32[]{:T(128)}) while((s32[]{:T(128)}, f32[3,2048]{1,0:T(4,128)S(1)}, f32[3,2048]{1,0:T(4,128)S(1)}, bf16[3,30,2048]{2,1,0:T(8,128)(2,1)S(1)}, ...), condition=%wide.region_24.25_spmd, body=%wide.region_19.24_spmd.sunk | while | flops 272627712 | bytes 737377 | solution.py:98
  103.4 1.4 convert_reduce_fusion.27
  104.7 1.4 convert_reduce_fusion.26
  106.4 1.4 convert_reduce_fusion.27
  107.8 1.4 convert_reduce_fusion.26
  109.5 1.4 convert_reduce_fusion.27
  110.8 1.4 convert_reduce_fusion.26
  112.6 1.6 %collective-permute-start.18 = (bf16[3,4096]{1,0:T(4,128)(2,1)S(1)}, bf16[3,4096]{1,0:T(4,128)(2,1)S(1)}, u32[]{:S(2)}, u32[]{:S(2)}) collective-permute-start(bf16[3,4096]{1,0:T(4,128)(2,1)S(1)} %convert_element_type.58), channel_id=1, source_target_pairs={{0,1},{1,0},{2,3},{3,2},{4,5},{5,4},{6,7},{7,6},{8,9},{9,8},{10,11... | collective-permute-start | bytes 73736 | tf_op jit(solution)/shard_map/ppermute | solution.py:44
  114.2 30.6 %while.34 = (s32[]{:T(128)}, f32[3,4096]{1,0:T(4,128)S(1)}, bf16[3,30,4096]{2,1,0:T(8,128)(2,1)S(1)}, s32[]{:T(128)}, s32[]{:T(128)}) while((s32[]{:T(128)}, f32[3,4096]{1,0:T(4,128)S(1)}, bf16[3,30,4096]{2,1,0:T(8,128)(2,1)S(1)}, s32[]{:T(128)}, s32[]{:T(128)}) %tuple.68), condition=%wide.region_12.13_spmd, body=%wide.region_7.12_spmd.sunk | while | flops 1073750016 | bytes 1884229 | solution.py:81
  114.4 2.5 %convert_reduce_fusion.20 = f32[1024]{0:T(1024)S(1)} fusion(bf16[30,4096]{1,0:T(8,128)(2,1)S(1)} %dynamic-slice_bitcast_fusion.6), kind=kOutput, calls=%fused_computation.clone.1 | convolution fusion | flops 268434432 | bytes 331776 | tf_op jit(solution)/shard_map/while/body/eval_jaxpr/dot_general | solution.py:60
  116.9 2.4 %convert_reduce_fusion.21 = f32[1024]{0:T(1024)S(1)} fusion(bf16[30,4096]{1,0:T(8,128)(2,1)S(1)} %dynamic-slice_bitcast_fusion.6), kind=kOutput, calls=%fused_computation.1.clone.1 | convolution fusion | flops 268434432 | bytes 331776 | tf_op jit(solution)/shard_map/while/body/eval_jaxpr/dot_general | solution.py:60
  119.3 2.4 %convert_reduce_fusion.22 = f32[1024]{0:T(1024)S(1)} fusion(bf16[30,4096]{1,0:T(8,128)(2,1)S(1)} %dynamic-slice_bitcast_fusion.6), kind=kOutput, calls=%fused_computation.2.clone.1 | convolution fusion | flops 268434432 | bytes 331776 | tf_op jit(solution)/shard_map/while/body/eval_jaxpr/dot_general | solution.py:60
  121.8 2.5 %convert_reduce_fusion.23 = f32[1024]{0:T(1024)S(1)} fusion(bf16[30,4096]{1,0:T(8,128)(2,1)S(1)} %dynamic-slice_bitcast_fusion.6), kind=kOutput, calls=%fused_computation.3.clone.1 | convolution fusion | flops 268434432 | bytes 331776 | tf_op jit(solution)/shard_map/while/body/eval_jaxpr/dot_general | solution.py:60
  124.6 2.4 %convert_reduce_fusion.20 = f32[1024]{0:T(1024)S(1)} fusion(bf16[30,4096]{1,0:T(8,128)(2,1)S(1)} %dynamic-slice_bitcast_fusion.6), kind=kOutput, calls=%fused_computation.clone.1 | convolution fusion | flops 268434432 | bytes 331776 | tf_op jit(solution)/shard_map/while/body/eval_jaxpr/dot_general | solution.py:60
  127.0 2.5 %convert_reduce_fusion.21 = f32[1024]{0:T(1024)S(1)} fusion(bf16[30,4096]{1,0:T(8,128)(2,1)S(1)} %dynamic-slice_bitcast_fusion.6), kind=kOutput, calls=%fused_computation.1.clone.1 | convolution fusion | flops 268434432 | bytes 331776 | tf_op jit(solution)/shard_map/while/body/eval_jaxpr/dot_general | solution.py:60
  129.5 2.5 %convert_reduce_fusion.22 = f32[1024]{0:T(1024)S(1)} fusion(bf16[30,4096]{1,0:T(8,128)(2,1)S(1)} %dynamic-slice_bitcast_fusion.6), kind=kOutput, calls=%fused_computation.2.clone.1 | convolution fusion | flops 268434432 | bytes 331776 | tf_op jit(solution)/shard_map/while/body/eval_jaxpr/dot_general | solution.py:60
  131.9 2.5 %convert_reduce_fusion.23 = f32[1024]{0:T(1024)S(1)} fusion(bf16[30,4096]{1,0:T(8,128)(2,1)S(1)} %dynamic-slice_bitcast_fusion.6), kind=kOutput, calls=%fused_computation.3.clone.1 | convolution fusion | flops 268434432 | bytes 331776 | tf_op jit(solution)/shard_map/while/body/eval_jaxpr/dot_general | solution.py:60
  134.7 2.4 %convert_reduce_fusion.20 = f32[1024]{0:T(1024)S(1)} fusion(bf16[30,4096]{1,0:T(8,128)(2,1)S(1)} %dynamic-slice_bitcast_fusion.6), kind=kOutput, calls=%fused_computation.clone.1 | convolution fusion | flops 268434432 | bytes 331776 | tf_op jit(solution)/shard_map/while/body/eval_jaxpr/dot_general | solution.py:60
  137.1 2.5 %convert_reduce_fusion.21 = f32[1024]{0:T(1024)S(1)} fusion(bf16[30,4096]{1,0:T(8,128)(2,1)S(1)} %dynamic-slice_bitcast_fusion.6), kind=kOutput, calls=%fused_computation.1.clone.1 | convolution fusion | flops 268434432 | bytes 331776 | tf_op jit(solution)/shard_map/while/body/eval_jaxpr/dot_general | solution.py:60
  139.6 2.5 %convert_reduce_fusion.22 = f32[1024]{0:T(1024)S(1)} fusion(bf16[30,4096]{1,0:T(8,128)(2,1)S(1)} %dynamic-slice_bitcast_fusion.6), kind=kOutput, calls=%fused_computation.2.clone.1 | convolution fusion | flops 268434432 | bytes 331776 | tf_op jit(solution)/shard_map/while/body/eval_jaxpr/dot_general | solution.py:60
  142.0 2.5 %convert_reduce_fusion.23 = f32[1024]{0:T(1024)S(1)} fusion(bf16[30,4096]{1,0:T(8,128)(2,1)S(1)} %dynamic-slice_bitcast_fusion.6), kind=kOutput, calls=%fused_computation.3.clone.1 | convolution fusion | flops 268434432 | bytes 331776 | tf_op jit(solution)/shard_map/while/body/eval_jaxpr/dot_general | solution.py:60
  (125 shorter events, 24.0 us)
Async XLA Ops:
  0.0 23.1 %all-to-all-start = ((f32[16,1,3840]{2,1,0:T(1,128)}), f32[16,1,3840]{2,1,0:T(1,128)S(1)}, u32[]{:S(2)}, u32[]{:S(2)}) async-start(f32[16,1,3840]{2,1,0:T(1,128)} %bitcast.92), calls=%async_computation | async-start | bytes 491520 | tf_op jit(solution)/shard_map/all_to_all | solution.py:109
  7.4 9.7 %collective-permute-start = (f32[1,1,6400]{2,1,0:T(1,128)}, f32[1,1,6400]{2,1,0:T(1,128)S(1)}, u32[]{:S(2)}, u32[]{:S(2)}) collective-permute-start(f32[1,1,6400]{2,1,0:T(1,128)} %param.9), channel_id=1, source_target_pairs={{0,2},{2,4},{4,6},{6,8},{8,10},{10,12},{12,14},{14,16},{16,18},{18... | collective-permute-start | bytes 76808 | tf_op jit(solution)/shard_map/ppermute | solution.py:21
  7.8 9.3 %collective-permute-start.1 = (f32[1,1,6400]{2,1,0:T(1,128)}, f32[1,1,6400]{2,1,0:T(1,128)S(1)}, u32[]{:S(2)}, u32[]{:S(2)}) collective-permute-start(f32[1,1,6400]{2,1,0:T(1,128)} %param.9), channel_id=1, source_target_pairs={{0,30},{2,0},{4,2},{6,4},{8,6},{10,8},{12,10},{14,12},{16,14},{18,... | collective-permute-start | bytes 76808 | tf_op jit(solution)/shard_map/ppermute | solution.py:24
  17.2 6.0 %collective-permute-start.2 = (f32[1,1,6400]{2,1,0:T(1,128)S(1)}, f32[1,1,6400]{2,1,0:T(1,128)S(1)}, u32[]{:S(2)}, u32[]{:S(2)}) collective-permute-start(f32[1,1,6400]{2,1,0:T(1,128)S(1)} %collective-permute-done), channel_id=1, source_target_pairs={{0,2},{2,4},{4,6},{6,8},{8,10},{10,12},{12,14},{14,16},{16,18},{18... | collective-permute-start | bytes 76808 | tf_op jit(solution)/shard_map/ppermute | solution.py:21
  17.2 8.3 %collective-permute-start.3 = (f32[1,1,6400]{2,1,0:T(1,128)S(1)}, f32[1,1,6400]{2,1,0:T(1,128)S(1)}, u32[]{:S(2)}, u32[]{:S(2)}) collective-permute-start(f32[1,1,6400]{2,1,0:T(1,128)S(1)} %collective-permute-done.1), channel_id=1, source_target_pairs={{0,30},{2,0},{4,2},{6,4},{8,6},{10,8},{12,10},{14,12},{16,14},{18,... | collective-permute-start | bytes 76808 | tf_op jit(solution)/shard_map/ppermute | solution.py:24
  23.1 6.8 %collective-permute-start.4 = (f32[1,1,6400]{2,1,0:T(1,128)S(1)}, f32[1,1,6400]{2,1,0:T(1,128)S(1)}, u32[]{:S(2)}, u32[]{:S(2)}) collective-permute-start(f32[1,1,6400]{2,1,0:T(1,128)S(1)} %collective-permute-done.2), channel_id=1, source_target_pairs={{0,2},{2,4},{4,6},{6,8},{8,10},{10,12},{12,14},{14,16},{16,18},{18... | collective-permute-start | bytes 76808 | tf_op jit(solution)/shard_map/ppermute | solution.py:21
  23.7 30.7 %copy-start.1 = (f32[1,1,6400]{2,1,0:T(1,128)S(1)}, f32[1,1,6400]{2,1,0:T(1,128)}, u32[]{:S(2)}) copy-start(f32[1,1,6400]{2,1,0:T(1,128)} %param.9) | copy-start | bytes 76804
  24.2 41.2 %collective-permute-start.16 = (f32[15,4096]{1,0:T(8,128)S(1)}, f32[15,4096]{1,0:T(8,128)S(1)}, u32[]{:S(2)}, u32[]{:S(2)}) collective-permute-start(f32[15,4096]{1,0:T(8,128)S(1)} %bitcast.85), channel_id=1, source_target_pairs={{0,2},{2,4},{4,6},{6,8},{8,10},{10,12},{12,14},{14,16},{16,18},{18... | collective-permute-start | bytes 737288 | tf_op jit(solution)/shard_map/ppermute | solution.py:34
  25.5 6.0 %collective-permute-start.5 = (f32[1,1,6400]{2,1,0:T(1,128)S(1)}, f32[1,1,6400]{2,1,0:T(1,128)S(1)}, u32[]{:S(2)}, u32[]{:S(2)}) collective-permute-start(f32[1,1,6400]{2,1,0:T(1,128)S(1)} %collective-permute-done.3), channel_id=1, source_target_pairs={{0,30},{2,0},{4,2},{6,4},{8,6},{10,8},{12,10},{14,12},{16,14},{18,... | collective-permute-start | bytes 76808 | tf_op jit(solution)/shard_map/ppermute | solution.py:24
  30.0 6.0 %collective-permute-start.6 = (f32[1,1,6400]{2,1,0:T(1,128)S(1)}, f32[1,1,6400]{2,1,0:T(1,128)S(1)}, u32[]{:S(2)}, u32[]{:S(2)}) collective-permute-start(f32[1,1,6400]{2,1,0:T(1,128)S(1)} %collective-permute-done.4), channel_id=1, source_target_pairs={{0,2},{2,4},{4,6},{6,8},{8,10},{10,12},{12,14},{14,16},{16,18},{18... | collective-permute-start | bytes 76808 | tf_op jit(solution)/shard_map/ppermute | solution.py:21
  31.5 6.0 %collective-permute-start.7 = (f32[1,1,6400]{2,1,0:T(1,128)S(1)}, f32[1,1,6400]{2,1,0:T(1,128)S(1)}, u32[]{:S(2)}, u32[]{:S(2)}) collective-permute-start(f32[1,1,6400]{2,1,0:T(1,128)S(1)} %collective-permute-done.5), channel_id=1, source_target_pairs={{0,30},{2,0},{4,2},{6,4},{8,6},{10,8},{12,10},{14,12},{16,14},{18,... | collective-permute-start | bytes 76808 | tf_op jit(solution)/shard_map/ppermute | solution.py:24
  35.9 6.0 %collective-permute-start.8 = (f32[1,1,6400]{2,1,0:T(1,128)S(1)}, f32[1,1,6400]{2,1,0:T(1,128)S(1)}, u32[]{:S(2)}, u32[]{:S(2)}) collective-permute-start(f32[1,1,6400]{2,1,0:T(1,128)S(1)} %collective-permute-done.6), channel_id=1, source_target_pairs={{0,2},{2,4},{4,6},{6,8},{8,10},{10,12},{12,14},{14,16},{16,18},{18... | collective-permute-start | bytes 76808 | tf_op jit(solution)/shard_map/ppermute | solution.py:21
  37.4 6.1 %collective-permute-start.9 = (f32[1,1,6400]{2,1,0:T(1,128)S(1)}, f32[1,1,6400]{2,1,0:T(1,128)S(1)}, u32[]{:S(2)}, u32[]{:S(2)}) collective-permute-start(f32[1,1,6400]{2,1,0:T(1,128)S(1)} %collective-permute-done.7), channel_id=1, source_target_pairs={{0,30},{2,0},{4,2},{6,4},{8,6},{10,8},{12,10},{14,12},{16,14},{18,... | collective-permute-start | bytes 76808 | tf_op jit(solution)/shard_map/ppermute | solution.py:24
  41.9 6.1 %collective-permute-start.10 = (f32[1,1,6400]{2,1,0:T(1,128)S(1)}, f32[1,1,6400]{2,1,0:T(1,128)S(1)}, u32[]{:S(2)}, u32[]{:S(2)}) collective-permute-start(f32[1,1,6400]{2,1,0:T(1,128)S(1)} %collective-permute-done.8), channel_id=1, source_target_pairs={{0,2},{2,4},{4,6},{6,8},{8,10},{10,12},{12,14},{14,16},{16,18},{18... | collective-permute-start | bytes 76808 | tf_op jit(solution)/shard_map/ppermute | solution.py:21
  42.2 23.2 %collective-permute-start.15 = (f32[10,4096]{1,0:T(8,128)S(1)}, f32[10,4096]{1,0:T(8,128)S(1)}, u32[]{:S(2)}, u32[]{:S(2)}) collective-permute-start(f32[10,4096]{1,0:T(8,128)S(1)} %bitcast.91), channel_id=1, source_target_pairs={{0,4},{2,6},{4,8},{6,10},{8,12},{10,14},{12,16},{14,18},{16,20},{1... | collective-permute-start | bytes 491528 | tf_op jit(solution)/shard_map/ppermute | solution.py:34
  43.5 6.0 %collective-permute-start.11 = (f32[1,1,6400]{2,1,0:T(1,128)S(1)}, f32[1,1,6400]{2,1,0:T(1,128)S(1)}, u32[]{:S(2)}, u32[]{:S(2)}) collective-permute-start(f32[1,1,6400]{2,1,0:T(1,128)S(1)} %collective-permute-done.9), channel_id=1, source_target_pairs={{0,30},{2,0},{4,2},{6,4},{8,6},{10,8},{12,10},{14,12},{16,14},{18,... | collective-permute-start | bytes 76808 | tf_op jit(solution)/shard_map/ppermute | solution.py:24
  48.0 6.1 %collective-permute-start.12 = (f32[1,1,6400]{2,1,0:T(1,128)S(1)}, f32[1,1,6400]{2,1,0:T(1,128)S(1)}, u32[]{:S(2)}, u32[]{:S(2)}) collective-permute-start(f32[1,1,6400]{2,1,0:T(1,128)S(1)} %collective-permute-done.10), channel_id=1, source_target_pairs={{0,2},{2,4},{4,6},{6,8},{8,10},{10,12},{12,14},{14,16},{16,18},{18... | collective-permute-start | bytes 76808 | tf_op jit(solution)/shard_map/ppermute | solution.py:21
  49.5 13.6 %collective-permute-start.13 = (f32[1,1,6400]{2,1,0:T(1,128)S(1)}, f32[1,1,6400]{2,1,0:T(1,128)S(1)}, u32[]{:S(2)}, u32[]{:S(2)}) collective-permute-start(f32[1,1,6400]{2,1,0:T(1,128)S(1)} %collective-permute-done.11), channel_id=1, source_target_pairs={{0,30},{2,0},{4,2},{6,4},{8,6},{10,8},{12,10},{14,12},{16,14},{18,... | collective-permute-start | bytes 76808 | tf_op jit(solution)/shard_map/ppermute | solution.py:24
  54.1 9.7 %collective-permute-start.14 = (f32[1,1,6400]{2,1,0:T(1,128)S(1)}, f32[1,1,6400]{2,1,0:T(1,128)S(1)}, u32[]{:S(2)}, u32[]{:S(2)}) collective-permute-start(f32[1,1,6400]{2,1,0:T(1,128)S(1)} %collective-permute-done.12), channel_id=1, source_target_pairs={{0,2},{2,4},{4,6},{6,8},{8,10},{10,12},{12,14},{14,16},{16,18},{18... | collective-permute-start | bytes 76808 | tf_op jit(solution)/shard_map/ppermute | solution.py:21
  74.6 1.6 %copy-start = (f32[3,4096]{1,0:T(4,128)S(1)}, f32[3,4096]{1,0:T(4,128)}, u32[]{:S(2)}) copy-start(f32[3,4096]{1,0:T(4,128)} %get-tuple-element.128) | copy-start | bytes 147460
  78.6 15.5 %collective-permute-start.17 = (bf16[3,30,4096]{2,1,0:T(8,128)(2,1)S(1)}, bf16[3,30,4096]{2,1,0:T(8,128)(2,1)S(1)}, u32[]{:S(2)}, u32[]{:S(2)}) collective-permute-start(bf16[3,30,4096]{2,1,0:T(8,128)(2,1)S(1)} %multiply_convert_fusion), channel_id=1, source_target_pairs={{0,1},{1,0},{2,3},{3,2},{4,5},{5,4},{6,7},{7,6},{8,9},{9,8},{10,11... | collective-permute-start | bytes 2211848 | tf_op jit(solution)/shard_map/ppermute | solution.py:44
  112.6 32.2 %collective-permute-start.18 = (bf16[3,4096]{1,0:T(4,128)(2,1)S(1)}, bf16[3,4096]{1,0:T(4,128)(2,1)S(1)}, u32[]{:S(2)}, u32[]{:S(2)}) collective-permute-start(bf16[3,4096]{1,0:T(4,128)(2,1)S(1)} %convert_element_type.58), channel_id=1, source_target_pairs={{0,1},{1,0},{2,3},{3,2},{4,5},{5,4},{6,7},{7,6},{8,9},{9,8},{10,11... | collective-permute-start | bytes 73736 | tf_op jit(solution)/shard_map/ppermute | solution.py:44
